TPU v7x, 32 devices: a whole 2x2x4 slice. The times are simulated.
32 devices in a mesh: row: 4 (over y, x), col: 8 (over z, core).
Axes of the slice: x: 2, y: 2, z: 4, core: 2. Of those that a mesh axis runs over, the one named last changes fastest.
Arguments:
- density: bfloat16 [2048, 2048], P('row', 'col'), may hold values from -0.125 to 0.125
- density_mask: int32 [16, 16], P('row', 'col'), may hold values from 0 to 1, as said below
- response: bfloat16 [2, 2048, 2048], P(None, 'row', 'col'), may hold values from -6 to 6
- response_mask: int32 [2, 16, 16], P(None, 'row', 'col'), may hold values from 0 to 1, as said below
- filter_mask: int32 [16, 16], P('row', 'col'), may hold values from 0 to 1, as said below
Outputs:
- product: bfloat16 [2, 2048, 2048], P(None, 'row', 'col')
Inputs may be any that keep to these rules, and one draw needn't show every extreme that they name: `density_mask`: diagonal blocks are always nonzero; blocks within cyclic block distance 2 of the diagonal are more often nonzero than blocks further out; whole block rows and whole block columns may be nonzero. `response_mask`: for each direction, diagonal blocks are always nonzero; blocks within cyclic block distance 2 of the diagonal are more often nonzero than blocks further out; whole block rows and whole block columns may be nonzero. `filter_mask`: diagonal blocks are always kept; blocks within cyclic block distance 2 * 2 of the diagonal are more often kept than blocks further out; whole block rows and whole block columns may be kept.
All inputs are finite; a program needn't handle non-finite values.
Results may differ from a plain program's by a relative error of at most 0.001.
Values may be sent and summed in bfloat16 or wider, within the bound.
A program may use at most 128 MiB of HBM per device.

v0:
```python
import jax
import jax.numpy as jnp
from jax import lax
from jax.sharding import PartitionSpec as P


def expand_blocks(values, mask, blocksize):
    lead = values.shape[:-2]
    height = values.shape[-2] // blocksize
    width = values.shape[-1] // blocksize
    shaped = values.reshape(lead + (height, blocksize, width, blocksize))
    scaled = shaped * mask.astype(values.dtype)[..., :, None, :, None]
    return scaled.reshape(values.shape)


def body(density, density_mask, response, response_mask, filter_mask):
    blocksize = density.shape[1] // density_mask.shape[1]
    masked_density = expand_blocks(density, density_mask, blocksize)
    masked_response = expand_blocks(response, response_mask, blocksize)
    density_full = lax.all_gather(masked_density, "col", axis=1, tiled=True)
    result = jnp.einsum(
        "ik,dkj->dij",
        density_full,
        lax.all_gather(masked_response, "row", axis=1, tiled=True),
        preferred_element_type=jnp.float32,
    )
    return expand_blocks(result, filter_mask, blocksize).astype(jnp.bfloat16)


def solution(mesh):
    in_specs = (
        P("row", "col"),
        P("row", "col"),
        P(None, "row", "col"),
        P(None, "row", "col"),
        P("row", "col"),
    )
    out_specs = P(None, "row", "col")
    return jax.shard_map(body, mesh=mesh, in_specs=in_specs, out_specs=out_specs, check_vma=False)
```

profile of v0, /device:TPU:9, one launch (start us, length us, event | category | flops | bytes accessed | tf_op | source)
XLA Modules:
  0.0 92.0 jit_solution(6940822390799597102)
XLA Ops:
  6.5 0.0 all-gather.3.cloned.1.call-start
  6.5 0.7 convert_element_type.12
  7.2 0.2 mul.35
  7.4 0.0 copy-start.2
  7.4 0.0 copy-start
  7.5 0.2 mul.36
  7.7 0.0 copy-start.1
  7.7 1.3 %copy.6 = bf16[2,512,256]{1,2,0:T(8,128)(2,1)S(1)} copy(bf16[2,512,256]{2,1,0:T(8,128)(2,1)} %param.7) | data formatting | bytes 1048576 | tf_op args[2]
  8.9 0.9 %mul.37 = bf16[2,512,256]{1,2,0:T(8,128)(2,1)} multiply(bf16[2,512,256]{1,2,0:T(8,128)(2,1)S(1)} %copy.6, bf16[2,512,256]{1,2,0:T(8,128)(2,1)S(1)} %mul.36) | non-fusion elementwise | flops 262144 | bytes 1572864 | tf_op jit(solution)/shard_map/mul | solution.py:12
  9.9 0.0 all-gather.3.cloned.1.call-update
  9.9 0.0 all-gather.5.cloned.1.call-start
  9.9 0.0 copy-done.2
  10.0 0.1 copy.7
  10.1 0.2 mul.38
  10.3 0.0 copy-done
  10.3 0.8 bitcast_multiply_fusion
  11.0 0.0 all-gather.5.cloned.1.call-update
  11.1 0.0 copy-done.1
  11.1 0.1 mul.41
  11.3 34.8 %all-gather.3.cloned.1.call-done = bf16[2,2048,256]{1,2,0:T(8,128)(2,1)} async-done(((bf16[2,512,256]{1,2,0:T(8,128)(2,1)}), bf16[2,2048,256]{1,2,0:T(8,128)(2,1)}) %all-gather.3.cloned.1.call-update) | async-done | bytes 2097168 | tf_op jit(solution)/shard_map/all_gather | solution.py:24
  46.1 34.6 %all-gather.5.cloned.1.call-done = bf16[512,2048]{1,0:T(8,128)(2,1)} async-done(((bf16[512,256]{1,0:T(8,128)(2,1)}), bf16[512,2048]{1,0:T(8,128)(2,1)}) %all-gather.5.cloned.1.call-update) | async-done | bytes 2097168 | tf_op jit(solution)/shard_map/all_gather | solution.py:20
  80.6 3.5 %fusion.8 = bf16[2,512,256]{1,2,0:T(8,128)(2,1)S(1)} fusion(bf16[2,2048,256]{1,2,0:T(8,128)(2,1)} %all-gather.3.cloned.1.call-done, bf16[512,2048]{1,0:T(8,128)(2,1)} %all-gather.5.cloned.1.call-done, f32[512,256]{0,1:T(8,128)S(1)} %bitcast.31), kind=kOutput, calls=%fused_computation.4 | convolution fusion | flops 1074266112 | bytes 5242880 | tf_op jit(solution)/shard_map/ik,dkj->dij/dot_general | solution.py:21
  84.2 1.0 %copy.8 = bf16[2,512,256]{2,1,0:T(8,128)(2,1)} copy(bf16[2,512,256]{1,2,0:T(8,128)(2,1)S(1)} %fusion.8) | data formatting | bytes 1048576 | tf_op jit(solution)/shard_map/convert_element_type | solution.py:27
  (3 shorter events, 0.0 us)
Async XLA Ops:
  6.5 39.5 %all-gather.3.cloned.1.call-start = ((), (), s32[]{:S(2)}) async-start(), calls=%async_computation | async-start | bytes 2621440 | tf_op jit(solution)/shard_map/all_gather | solution.py:24
  7.4 2.5 %copy-start.2 = (s32[4,2]{0,1:T(2,128)S(1)}, s32[4,2]{0,1:T(2,128)}, u32[]{:S(2)}) copy-start(s32[4,2]{0,1:T(2,128)} %param.6) | copy-start | bytes 100
  7.4 2.8 %copy-start = (bf16[512,256]{1,0:T(8,128)(2,1)S(1)}, bf16[512,256]{1,0:T(8,128)(2,1)}, u32[]{:S(2)}) copy-start(bf16[512,256]{1,0:T(8,128)(2,1)} %param.5) | copy-start | bytes 786436
  7.7 3.4 %copy-start.1 = (s32[4,2]{0,1:T(2,128)S(1)}, s32[4,2]{0,1:T(2,128)}, u32[]{:S(2)}) copy-start(s32[4,2]{0,1:T(2,128)} %param.9) | copy-start | bytes 100
  9.9 70.8 %all-gather.5.cloned.1.call-start = ((), (), s32[]{:S(2)}) async-start(), calls=%async_computation.1 | async-start | bytes 2359296 | tf_op jit(solution)/shard_map/all_gather | solution.py:20
Sparse Core Ops, SparseCore 0:
  10.0 36.0 all-gather.2
  47.7 32.9 all-gather.4
where the time goes:
time: 92.2 us; the launch traced here: 92 us
  waiting for transfers between devices  69.4 us (75%)
  between operations  13.5 us (15%)
  matrix products  3.5 us (4%)
  local copies, waits for them, and re-layouts  3.17 us (3%)
  other arithmetic  2.37 us (3%)
    all_gather x1, waiting for transfers between devices, body(): lax.all_gather(masked_response, 'row', axis=1, tiled=True)  34.8 us
    all_gather x1, waiting for transfers between devices, body(): density_full = lax.all_gather(masked_density, 'col', axis=1, tiled=True)  34.6 us
    dot_general x1, matrix products, body(): jnp.einsum('ik,dkj->dij', density_full, lax.all_gather(masked_response, '...  3.5 us
  transfers between devices with their start and end apart: 2, of which 2 were waited for; matrix products, arithmetic and copies ran while one was open for 1% of the time, Pallas kernels for 0%

commit v1 on v0

--- a/solution.py
+++ b/solution.py
@@ -14,15 +14,39 @@
 
 
 def body(density, density_mask, response, response_mask, filter_mask):
+
+    def fix_row(raw, matrix):
+        which_axis = "row"
+        outcome_arr, b_next, local_out = (
+            lax.axis_size(which_axis),
+            lax.axis_index(which_axis),
+            raw.shape[1],
+        )
+        buffers = [(jj, (jj + 1) % outcome_arr) for jj in range(outcome_arr)]
+        pool = [(jj, (jj - 1) % outcome_arr) for jj in range(outcome_arr)]
+        long_array = outcome_arr // 2
+        last = piece_out = raw
+        e_next = matrix(raw, b_next * local_out)
+        for j0 in tuple(range(1, long_array + 1)):
+            last = lax.ppermute(last, which_axis, buffers)
+            if j0 < outcome_arr - long_array:
+                piece_out = lax.ppermute(piece_out, which_axis, perm=pool)
+                e_next = e_next + matrix(piece_out, (b_next + j0) % outcome_arr * local_out)
+            e_next = e_next + matrix(last, (b_next - j0) % outcome_arr * local_out)
+        return e_next
+
     blocksize = density.shape[1] // density_mask.shape[1]
     masked_density = expand_blocks(density, density_mask, blocksize)
     masked_response = expand_blocks(response, response_mask, blocksize)
     density_full = lax.all_gather(masked_density, "col", axis=1, tiled=True)
-    result = jnp.einsum(
-        "ik,dkj->dij",
-        density_full,
-        lax.all_gather(masked_response, "row", axis=1, tiled=True),
-        preferred_element_type=jnp.float32,
+    result = fix_row(
+        masked_response,
+        lambda own_block, offset: jnp.einsum(
+            "ik,dkj->dij",
+            lax.dynamic_slice_in_dim(density_full, offset, own_block.shape[1], axis=1),
+            own_block,
+            preferred_element_type=jnp.float32,
+        ),
     )
     return expand_blocks(result, filter_mask, blocksize).astype(jnp.bfloat16)
 

time: 92.2 us -> 57.7 us (0.63)
  the two profiles are of different devices: /device:TPU:9 before, /device:TPU:0 now
where the time goes in v1:
time: 57.7 us; the launch traced here: 57.5 us
  waiting for transfers between devices  30.4 us (53%)
  between operations  13.5 us (23%)
  starting transfers between devices  5.11 us (9%)
  other arithmetic  3.26 us (6%)
  matrix products  3.08 us (5%)
  local copies, waits for them, and re-layouts  2.19 us (4%)
    ppermute x2, waiting for transfers between devices, fix_row(): last = lax.ppermute(last, which_axis, buffers)  16.1 us
    all_gather x1, waiting for transfers between devices, body(): density_full = lax.all_gather(masked_density, 'col', axis=1, tiled=True)  14.2 us
    ppermute x2, starting transfers between devices, fix_row(): last = lax.ppermute(last, which_axis, buffers)  4.08 us
    dot_general x4, matrix products, body(): jnp.einsum('ik,dkj->dij', lax.dynamic_slice_in_dim(density_full, offset,...  3.08 us
    mul x2, other arithmetic, expand_blocks(): scaled = shaped * mask.astype(values.dtype)[..., :, None, :, None]  1.83 us
    convert_element_type x3, other arithmetic, expand_blocks(): scaled = shaped * mask.astype(values.dtype)[..., :, None, :, None]  1.43 us
  transfers between devices with their start and end apart: 4, of which 3 were waited for; matrix products, arithmetic and copies ran while one was open for 7% of the time, Pallas kernels for 0%

profile of v1, /device:TPU:0, one launch (start us, length us, event | category | flops | bytes accessed | tf_op | source)
XLA Modules:
  0.0 57.5 jit_solution(16628742426379531216)
XLA Ops:
  6.5 0.7 %convert_element_type.13 = bf16[4,2]{0,1:T(2,128)(2,1)S(1)} convert(s32[4,2]{0,1:T(2,128)} %param.6) | non-fusion elementwise | flops 8 | bytes 48 | tf_op jit(solution)/shard_map/convert_element_type | solution.py:12
  7.3 0.1 copy.7
  7.4 0.2 mul.50
  7.6 1.7 %bitcast_multiply_fusion = bf16[512,256]{1,0:T(8,128)(2,1)} fusion(bf16[512,256]{1,0:T(8,128)(2,1)} %param.5, bf16[64,8,2,128]{3,2,1,0:T(2,128)(2,1)S(1)} %bitcast.37), kind=kLoop, calls=%fused_computation.16 | loop fusion | flops 131072 | bytes 786432 | tf_op jit(solution)/shard_map/mul | solution.py:12
  9.3 0.0 all-gather.2.cloned.1.call-update
  9.3 0.7 %convert_element_type.12 = bf16[2,4,2]{1,2,0:T(2,128)(2,1)S(1)} convert(s32[2,4,2]{1,2,0:T(2,128)} %param.8) | non-fusion elementwise | flops 16 | bytes 96 | tf_op jit(solution)/shard_map/convert_element_type | solution.py:12
  10.0 0.2 mul.47
  10.2 0.2 mul.48
  10.4 0.2 copy.6
  10.6 0.1 mul.49
  10.8 3.0 %collective-permute-start.1 = (bf16[2,512,256]{1,2,0:T(8,128)(2,1)S(1)}, bf16[2,512,256]{1,2,0:T(8,128)(2,1)S(1)}, u32[]{:S(2)}, u32[]{:S(2)}) collective-permute-start(bf16[2,512,256]{1,2,0:T(8,128)(2,1)S(1)} %mul.49), channel_id=1, source_target_pairs={{0,8},{8,16},{16,24},{24,0},{1,9},{9,17},{17,25},{25,1},{2,10},{10... | collective-permute-start | bytes 1572872 | tf_op jit(solution)/shard_map/ppermute | solution.py:31
  13.8 1.0 %collective-permute-start = (bf16[2,512,256]{1,2,0:T(8,128)(2,1)S(1)}, bf16[2,512,256]{1,2,0:T(8,128)(2,1)S(1)}, u32[]{:S(2)}, u32[]{:S(2)}) collective-permute-start(bf16[2,512,256]{1,2,0:T(8,128)(2,1)S(1)} %mul.49), channel_id=1, source_target_pairs={{0,24},{8,0},{16,8},{24,16},{1,25},{9,1},{17,9},{25,17},{2,26},{10... | collective-permute-start | bytes 1572872 | tf_op jit(solution)/shard_map/ppermute | solution.py:33
  14.8 0.1 mul.57
  15.0 12.5 %collective-permute-done.1 = bf16[2,512,256]{1,2,0:T(8,128)(2,1)S(1)} collective-permute-done((bf16[2,512,256]{1,2,0:T(8,128)(2,1)S(1)}, bf16[2,512,256]{1,2,0:T(8,128)(2,1)S(1)}, u32[]{:S(2)}, u32[]{:S(2)}) %collective-permute-start.1) | collective-permute-done | bytes 524320 | tf_op jit(solution)/shard_map/ppermute | solution.py:31
  27.5 1.1 %collective-permute-start.2 = (bf16[2,512,256]{1,2,0:T(8,128)(2,1)S(1)}, bf16[2,512,256]{1,2,0:T(8,128)(2,1)S(1)}, u32[]{:S(2)}, u32[]{:S(2)}) collective-permute-start(bf16[2,512,256]{1,2,0:T(8,128)(2,1)S(1)} %collective-permute-done.1), channel_id=1, source_target_pairs={{0,8},{8,16},{16,24},{24,0},{1,9},{9,17},{17,25},{25,1},{2,10},{10... | collective-permute-start | bytes 1572872 | tf_op jit(solution)/shard_map/ppermute | solution.py:31
  28.6 14.2 %all-gather.2.cloned.1.call-done = bf16[512,2048]{1,0:T(8,128)(2,1)} async-done(((bf16[512,256]{1,0:T(8,128)(2,1)}), bf16[512,2048]{1,0:T(8,128)(2,1)}) %all-gather.2.cloned.1.call-update) | async-done | bytes 2097168 | tf_op jit(solution)/shard_map/all_gather | solution.py:41
  42.8 1.7 %fusion.6 = f32[2,256,512]{2,1,0:T(8,128)S(1)} fusion(bf16[2,512,256]{1,2,0:T(8,128)(2,1)S(1)} %mul.49, bf16[512,2048]{1,0:T(8,128)(2,1)} %all-gather.2.cloned.1.call-done, s32[]{:T(128)S(6)} %select_n.27), kind=kOutput, calls=%fused_computation.10 | convolution fusion | flops 268435456 | bytes 2097156 | tf_op jit(solution)/shard_map/ik,dkj->dij/dot_general | solution.py:44
  44.5 0.0 collective-permute-done
  44.5 0.1 copy-done
  44.6 0.5 convolution_add_fusion.2
  45.0 0.5 convolution_add_fusion.1
  45.5 3.6 %collective-permute-done.2 = bf16[2,512,256]{1,2,0:T(8,128)(2,1)S(1)} collective-permute-done((bf16[2,512,256]{1,2,0:T(8,128)(2,1)S(1)}, bf16[2,512,256]{1,2,0:T(8,128)(2,1)S(1)}, u32[]{:S(2)}, u32[]{:S(2)}) %collective-permute-start.2) | collective-permute-done | bytes 524320 | tf_op jit(solution)/shard_map/ppermute | solution.py:31
  49.2 0.5 fusion.2
  49.6 1.0 %copy.8 = bf16[2,512,256]{2,1,0:T(8,128)(2,1)} copy(bf16[2,512,256]{1,2,0:T(8,128)(2,1)S(1)} %fusion.2) | data formatting | bytes 1048576 | tf_op jit(solution)/shard_map/convert_element_type | solution.py:51
  (8 shorter events, 0.0 us)
Async XLA Ops:
  6.5 3.9 %copy-start.1 = (bf16[2,512,256]{2,1,0:T(8,128)(2,1)S(1)}, bf16[2,512,256]{2,1,0:T(8,128)(2,1)}, u32[]{:S(2)}) copy-start(bf16[2,512,256]{2,1,0:T(8,128)(2,1)} %param.7) | copy-start | bytes 1572868
  6.5 36.3 %all-gather.2.cloned.1.call-start = ((), (), s32[]{:S(2)}) async-start(), calls=%async_computation | async-start | bytes 2359296 | tf_op jit(solution)/shard_map/all_gather | solution.py:41
  10.0 4.8 %copy-start.2 = (s32[4,2]{0,1:T(2,128)S(1)}, s32[4,2]{0,1:T(2,128)}, u32[]{:S(2)}) copy-start(s32[4,2]{0,1:T(2,128)} %param.9) | copy-start | bytes 100
  10.8 16.7 %collective-permute-start.1 = (bf16[2,512,256]{1,2,0:T(8,128)(2,1)S(1)}, bf16[2,512,256]{1,2,0:T(8,128)(2,1)S(1)}, u32[]{:S(2)}, u32[]{:S(2)}) collective-permute-start(bf16[2,512,256]{1,2,0:T(8,128)(2,1)S(1)} %mul.49), channel_id=1, source_target_pairs={{0,8},{8,16},{16,24},{24,0},{1,9},{9,17},{17,25},{25,1},{2,10},{10... | collective-permute-start | bytes 1572872 | tf_op jit(solution)/shard_map/ppermute | solution.py:31
  13.8 30.7 %collective-permute-start = (bf16[2,512,256]{1,2,0:T(8,128)(2,1)S(1)}, bf16[2,512,256]{1,2,0:T(8,128)(2,1)S(1)}, u32[]{:S(2)}, u32[]{:S(2)}) collective-permute-start(bf16[2,512,256]{1,2,0:T(8,128)(2,1)S(1)} %mul.49), channel_id=1, source_target_pairs={{0,24},{8,0},{16,8},{24,16},{1,25},{9,1},{17,9},{25,17},{2,26},{10... | collective-permute-start | bytes 1572872 | tf_op jit(solution)/shard_map/ppermute | solution.py:33
  27.5 21.6 %collective-permute-start.2 = (bf16[2,512,256]{1,2,0:T(8,128)(2,1)S(1)}, bf16[2,512,256]{1,2,0:T(8,128)(2,1)S(1)}, u32[]{:S(2)}, u32[]{:S(2)}) collective-permute-start(bf16[2,512,256]{1,2,0:T(8,128)(2,1)S(1)} %collective-permute-done.1), channel_id=1, source_target_pairs={{0,8},{8,16},{16,24},{24,0},{1,9},{9,17},{17,25},{25,1},{2,10},{10... | collective-permute-start | bytes 1572872 | tf_op jit(solution)/shard_map/ppermute | solution.py:31
  42.8 1.8 %copy-start = (bf16[512,2048]{1,0:T(8,128)(2,1)S(1)}, bf16[512,2048]{1,0:T(8,128)(2,1)}, u32[]{:S(2)}) copy-start(bf16[512,2048]{1,0:T(8,128)(2,1)} %all-gather.2.cloned.1.call-done) | copy-start | bytes 6291460
Sparse Core Ops, SparseCore 0:
  9.4 33.3 all-gather.1

commit v2 on v0

--- a/solution.py
+++ b/solution.py
@@ -17,7 +17,11 @@
     blocksize = density.shape[1] // density_mask.shape[1]
     masked_density = expand_blocks(density, density_mask, blocksize)
     masked_response = expand_blocks(response, response_mask, blocksize)
-    density_full = lax.all_gather(masked_density, "col", axis=1, tiled=True)
+
+    def _measure_arrays(my_data):
+        return jnp.concatenate(lax.all_gather(my_data, "col"), axis=1)
+
+    density_full = _measure_arrays(masked_density)
     result = jnp.einsum(
         "ik,dkj->dij",
         density_full,

time: 92.2 us -> 89.2 us (0.967)
  the two profiles are of different devices: /device:TPU:9 before, /device:TPU:0 now
where the time goes in v2:
time: 89.2 us; the launch traced here: 89 us
  waiting for transfers between devices  60.7 us (68%)
  between operations  13.5 us (15%)
  local copies, waits for them, and re-layouts  7.23 us (8%)
  other arithmetic  4.07 us (5%)
  matrix products  3.5 us (4%)
    all_gather x1, waiting for transfers between devices, body(): lax.all_gather(masked_response, 'row', axis=1, tiled=True)  31.2 us
    all_gather x1, waiting for transfers between devices, _measure_arrays(): return jnp.concatenate(lax.all_gather(my_data, 'col'), axis=1)  29.5 us
    dot_general x1, matrix products, body(): jnp.einsum('ik,dkj->dij', density_full, lax.all_gather(masked_response, '...  3.5 us
    all_gather x1, local copies, waits for them, and re-layouts, _measure_arrays(): return jnp.concatenate(lax.all_gather(my_data, 'col'), axis=1)  2.76 us
    mul x2, other arithmetic, expand_blocks(): scaled = shaped * mask.astype(values.dtype)[..., :, None, :, None]  2.64 us
    reshape x1, local copies, waits for them, and re-layouts, _measure_arrays(): return jnp.concatenate(lax.all_gather(my_data, 'col'), axis=1)  2.35 us
  transfers between devices with their start and end apart: 2, of which 2 were waited for; matrix products, arithmetic and copies ran while one was open for 8% of the time, Pallas kernels for 0%

profile of v2, /device:TPU:0, one launch (start us, length us, event | category | flops | bytes accessed | tf_op | source)
XLA Modules:
  0.0 89.0 jit_solution(15275198282727554696)
XLA Ops:
  6.5 0.0 copy-start
  6.5 0.0 all-gather.6.cloned.1.call-start
  6.5 0.7 convert_element_type.13
  7.3 0.1 copy.7
  7.4 0.2 mul.41
  7.6 1.7 %bitcast_multiply_fusion = bf16[512,256]{1,0:T(8,128)(2,1)} fusion(bf16[512,256]{1,0:T(8,128)(2,1)} %param.5, bf16[64,8,2,128]{3,2,1,0:T(2,128)(2,1)S(1)} %bitcast.28), kind=kLoop, calls=%fused_computation.5 | loop fusion | flops 131072 | bytes 786432 | tf_op jit(solution)/shard_map/mul | solution.py:12
  9.3 0.0 all-gather.6.cloned.1.call-update
  9.3 0.0 all-gather.4.cloned.1.call-start
  9.4 0.7 convert_element_type.12
  10.1 0.2 mul.38
  10.3 0.0 copy-start.1
  10.3 0.2 mul.39
  10.5 0.0 copy-done
  10.5 0.2 copy.6
  10.7 0.9 %mul.40 = bf16[2,512,256]{1,2,0:T(8,128)(2,1)} multiply(bf16[2,512,256]{1,2,0:T(8,128)(2,1)S(1)} %copy.6, bf16[2,512,256]{1,2,0:T(8,128)(2,1)S(1)} %mul.39) | non-fusion elementwise | flops 262144 | bytes 1572864 | tf_op jit(solution)/shard_map/mul | solution.py:12
  11.7 0.0 all-gather.4.cloned.1.call-update
  11.7 0.0 copy-done.1
  11.7 0.1 mul.45
  11.9 29.5 %all-gather.6.cloned.1.call-done = bf16[4096,256]{1,0:T(8,128)(2,1)} async-done(((bf16[512,256]{1,0:T(8,128)(2,1)}), bf16[4096,256]{1,0:T(8,128)(2,1)}) %all-gather.6.cloned.1.call-update) | async-done | bytes 2097168 | tf_op jit(solution)/shard_map/all_gather | solution.py:22
  41.4 2.8 %copy.15 = bf16[8,512,256]{2,0,1:T(8,128)(2,1)S(1)} copy(bf16[8,512,256]{2,1,0:T(8,128)(2,1)} %bitcast.26) | data formatting | bytes 4194304 | tf_op jit(solution)/shard_map/all_gather | solution.py:22
  44.1 2.3 %reshape.25 = bf16[512,2048,1]{1,0,2:T(8,128)(2,1)} reshape(bf16[512,8,256]{2,1,0:T(8,128)(2,1)S(1)} %bitcast.25) | data formatting | bytes 4194304 | tf_op jit(solution)/shard_map/reshape | solution.py:22
  46.5 31.2 %all-gather.4.cloned.1.call-done = bf16[2,2048,256]{1,2,0:T(8,128)(2,1)} async-done(((bf16[2,512,256]{1,2,0:T(8,128)(2,1)}), bf16[2,2048,256]{1,2,0:T(8,128)(2,1)}) %all-gather.4.cloned.1.call-update) | async-done | bytes 2097168 | tf_op jit(solution)/shard_map/all_gather | solution.py:28
  77.7 3.5 %fusion.1 = bf16[2,512,256]{1,2,0:T(8,128)(2,1)S(1)} fusion(bf16[2,2048,256]{1,2,0:T(8,128)(2,1)} %all-gather.4.cloned.1.call-done, bf16[512,2048,1]{1,0,2:T(8,128)(2,1)} %reshape.25, f32[512,256]{0,1:T(8,128)S(1)} %bitcast.29), kind=kOutput, calls=%fused_computation.3 | convolution fusion | flops 1074266112 | bytes 5242880 | tf_op jit(solution)/shard_map/ik,dkj->dij/dot_general | solution.py:25
  81.2 1.0 %copy.9 = bf16[2,512,256]{2,1,0:T(8,128)(2,1)} copy(bf16[2,512,256]{1,2,0:T(8,128)(2,1)S(1)} %fusion.1) | data formatting | bytes 1048576 | tf_op jit(solution)/shard_map/convert_element_type | solution.py:31
  (2 shorter events, 0.0 us)
Async XLA Ops:
  6.5 4.0 %copy-start = (bf16[2,512,256]{2,1,0:T(8,128)(2,1)S(1)}, bf16[2,512,256]{2,1,0:T(8,128)(2,1)}, u32[]{:S(2)}) copy-start(bf16[2,512,256]{2,1,0:T(8,128)(2,1)} %param.7) | copy-start | bytes 1572868
  6.5 34.8 %all-gather.6.cloned.1.call-start = ((), (), s32[]{:S(2)}) async-start(), calls=%async_computation.1 | async-start | bytes 2359296 | tf_op jit(solution)/shard_map/all_gather | solution.py:22
  9.3 68.3 %all-gather.4.cloned.1.call-start = ((), (), s32[]{:S(2)}) async-start(), calls=%async_computation | async-start | bytes 2621440 | tf_op jit(solution)/shard_map/all_gather | solution.py:28
  10.3 1.4 %copy-start.1 = (s32[4,2]{0,1:T(2,128)S(1)}, s32[4,2]{0,1:T(2,128)}, u32[]{:S(2)}) copy-start(s32[4,2]{0,1:T(2,128)} %param.9) | copy-start | bytes 100
Sparse Core Ops, SparseCore 0:
  9.5 31.8 all-gather.5
  43.2 34.4 all-gather.3
